TPU v7x, 256 devices: a whole 4x4x8 slice. The times are simulated.
256 devices in a mesh: krow: 32 (over z, x_lo, core), kcol: 8 (over x_hi, y).
Axes of the slice: x: 4 (x_hi: 2, x_lo: 2; x = x_hi * 2 + x_lo), y: 4, z: 8, core: 2. Of those that a mesh axis runs over, the one named last changes fastest.
Arguments:
- green: bfloat16 [4, 2, 32, 16, 256, 256], P(None, None, 'krow', 'kcol'), may hold values from -6 to 6
- screened: float32 [32, 16, 65536], P(None, None, ('krow', 'kcol')), may hold values from 0.1 to 1
Outputs:
- sigma: bfloat16 [4, 2, 32, 16, 256, 256], P(None, None, 'krow', 'kcol')
- dressed: bfloat16 [4, 2, 32, 16, 256, 256], P(None, None, 'krow', 'kcol')
All inputs are finite; a program needn't handle non-finite values.
Results may differ from a plain program's by a relative error of at most 0.0053.
Values may be sent and summed in bfloat16 or wider, within the bound.
A program may use at most 64 MiB of HBM per device.

v0:
```python
import math

import jax
import jax.numpy as jnp
from jax import lax
from jax.experimental import pallas as pl
from jax.experimental.pallas import tpu as pltpu
from jax.sharding import PartitionSpec as P

MESH = pl.DeviceIdType.MESH
HALVES = 2
SPLIT_TABLE = True
SINE = [(-1) ** n * (math.pi / 16) ** (2 * n + 1) / math.factorial(2 * n + 1) for n in range(7)]


def place():
    row, col = lax.axis_index("krow"), lax.axis_index("kcol")
    z, x_low, core = row // 4, (row // 2) % 2, row % 2
    x_high, y = col // 4, col % 4
    return row, col, z, x_high * 2 + x_low, y, core


def for_peers(visit):
    _, _, z, x, y, core = place()
    z_rows = [((z + dz) % 8) * 4 for dz in (4, 1, 7, 2, 6, 3, 5, 0)]

    def group(step, first):
        offset = (step * 13) % 32
        x_to, y_to, core_to = (x + offset // 8) % 4, (y + (offset // 2) % 4) % 4, (core + offset % 2) % 2
        low, col = (x_to % 2) * 2 + core_to, (x_to // 2) * 4 + y_to
        for z_row in z_rows[: 7 if first else 8]:
            visit(z_row + low, col)

    group(0, True)

    def body(step, carry):
        group(step, False)
        return carry

    lax.fori_loop(1, 32, body, 0)


def kernel(
    green_hbm, screened_hbm, sigma, dressed,
    green, weights, factors, wide, packed, landed, middle, back,
    table, table_low, states, weighted, load_sem, send_sem, recv_sem,
):
    row, col = place()[:2]
    me = row * 8 + col

    barrier = pltpu.get_barrier_semaphore()
    loads = [
        pltpu.make_async_copy(green_hbm.at[pl.ds(h * 8, 8)], green.at[pl.ds(h * 8, 8)], load_sem.at[h])
        for h in range(HALVES)
    ]
    loads += [
        pltpu.make_async_copy(
            screened_hbm.at[:, pl.ds(side * 128, 128)], weights.at[side], load_sem.at[2 + side]
        )
        for side in range(2)
    ]
    for load in loads:
        load.start()
    for_peers(lambda r, c: pl.semaphore_signal(barrier, inc=1, device_id=(r, c), device_id_type=MESH))

    def pack(h):
        for j in range(8):
            for side in range(2):
                part = green[h * 8 + j, :, pl.ds(side * 128, 128)]
                wide[side, pl.ds(j, 256, stride=8), :] = part.astype(jnp.float32)

        def body(i, carry):
            for side in range(2):
                rows = wide[side, pl.ds(i * 256, 256), :].reshape(32, 8, 128)
                packed[h, pl.ds(i * 32, 32), :, pl.ds(side * 128, 128)] = rows.astype(jnp.bfloat16)
            return carry

        lax.fori_loop(0, 8, body, 0)

    def send(source, target, h, lane):
        target[h, me] = source[h, me]

        def one(r, c):
            pltpu.make_async_remote_copy(
                source.at[h, r * 8 + c], target.at[h, me], send_sem.at[lane], recv_sem.at[lane],
                device_id=(r, c), device_id_type=MESH,
            ).start()

        for_peers(one)

    def arrive(source, target, h, lane):
        pltpu.make_async_remote_copy(
            source.at[h, pl.ds(0, 255)], target.at[h, pl.ds(0, 255)], send_sem.at[lane], recv_sem.at[lane],
            device_id=(row, col), device_id_type=MESH,
        ).wait_recv()

    def leave(source, target, h, lane):
        pltpu.make_async_remote_copy(
            source.at[h, pl.ds(0, 255)], target.at[h, pl.ds(0, 255)], send_sem.at[lane], recv_sem.at[lane],
            device_id=(row, col), device_id_type=MESH,
        ).wait_send()

    def fill_tables():
        r = lax.broadcasted_iota(jnp.int32, (32, 1024), 0)
        k = lax.broadcasted_iota(jnp.int32, (32, 1024), 1)
        r_two, r_part = (r // 4) * 2 + r % 2, (r // 2) % 2
        k_one, k_two, k_part = k // 32, ((k // 4) % 8) * 2 + k % 2, (k // 2) % 2
        start = 2 * k_two * r_two + 8 * (k_part - r_part) + 48

        def body(one, carry):
            turn = (start + one * k_one) % 32
            t = (8 - jnp.abs(turn - 16)).astype(jnp.float32)
            square = t * t
            value = jnp.full_like(t, SINE[6])
            for c in SINE[5::-1]:
                value = value * square + c
            value = value * t
            high = value.astype(jnp.bfloat16)
            at = pl.ds(one * 32, 32)
            table[at, :] = high
            if SPLIT_TABLE:
                table_low[at, :] = (value - high.astype(jnp.float32)).astype(jnp.bfloat16)
            return carry

        lax.fori_loop(0, 32, body, 0)

    def fill_factors():
        for side in range(2):
            for low in range(2):
                rows = weights[side, pl.ds(low, 256, stride=2), :] * (1.0 / 512)
                factors[side, pl.ds(low, 256, stride=4), :] = -rows
                factors[side, pl.ds(2 + low, 256, stride=4), :] = rows

    def times_table(at, operand):
        product = jnp.dot(table[at, :], operand[...], preferred_element_type=jnp.float32)
        if SPLIT_TABLE:
            product = product + jnp.dot(table_low[at, :], operand[...], preferred_element_type=jnp.float32)
        return product

    def convolve(h):
        upper = lax.broadcasted_iota(jnp.int32, (8, 8, 256), 1) < 4

        def gather(i, carry):
            rows = landed[h, pl.ds(i * 16, 16)].astype(jnp.float32).reshape(8, 2, 8, 256)
            even, odd = rows[:, 0], rows[:, 1]
            at = pl.ds(i * 64, 64)
            zero = jnp.where(upper, even, pltpu.roll(odd, 4, 1))
            one = jnp.where(upper, pltpu.roll(even, 4, 1), odd)
            states[at, pl.ds(0, 256)] = zero.reshape(64, 256).astype(jnp.bfloat16)
            states[at, pl.ds(256, 256)] = one.reshape(64, 256).astype(jnp.bfloat16)
            return carry

        lax.fori_loop(0, 16, gather, 0)

        def forward(i, carry):
            at = pl.ds(i * 256, 256)
            product = times_table(at, states)
            for q in range(4):
                part = product[:, q * 128 : (q + 1) * 128] * factors[q % 2, at, :]
                weighted[at, pl.ds(q * 128, 128)] = part.astype(jnp.bfloat16)
            return carry

        lax.fori_loop(0, 4, forward, 0)

        index = lax.broadcasted_iota(jnp.int32, (32, 8, 256), 1)
        sign = jnp.where((index // 2) % 2 == 0, 1.0, -1.0)

        def inverse(i, carry):
            product = times_table(pl.ds(i * 256, 256), weighted)
            zero = product[:, :256].reshape(32, 8, 256) * sign
            one = product[:, 256:].reshape(32, 8, 256) * sign
            even = jnp.where(index < 4, zero, pltpu.roll(one, 4, 1))
            odd = jnp.where(index < 4, pltpu.roll(zero, 4, 1), one)
            both = jnp.stack((even, odd), 1).reshape(64, 8, 256)
            middle[h, pl.ds(i * 64, 64)] = both.astype(jnp.bfloat16)
            return carry

        lax.fori_loop(0, 4, inverse, 0)

    def finish(h):
        def unpack(i, carry):
            for side in range(2):
                rows = back[h, pl.ds(i * 32, 32), :, pl.ds(side * 128, 128)].astype(jnp.float32)
                wide[side, pl.ds(i * 256, 256), :] = rows.reshape(256, 128)
            return carry

        lax.fori_loop(0, 8, unpack, 0)
        for j in range(8):
            for side in range(2):
                rows = wide[side, pl.ds(j, 256, stride=8), :]
                sigma[h * 8 + j, :, pl.ds(side * 128, 128)] = rows.astype(jnp.bfloat16)

        def dot(a, b):
            return jnp.dot(a, b, preferred_element_type=jnp.float32)

        def one(i, carry):
            real = h * 8 + (i // 2) * 4 + i % 2
            imag = real + 2
            g_real, g_imag, s_real, s_imag = green[real], green[imag], sigma[real], sigma[imag]
            k_real = (dot(g_real, s_real) - dot(g_imag, s_imag)).astype(jnp.bfloat16)
            k_imag = (dot(g_real, s_imag) + dot(g_imag, s_real)).astype(jnp.bfloat16)
            c_real = dot(k_real, g_real) - dot(k_imag, g_imag)
            c_imag = dot(k_real, g_imag) + dot(k_imag, g_real)
            dressed[real] = (g_real.astype(jnp.float32) + c_real * (1.0 / 256)).astype(jnp.bfloat16)
            dressed[imag] = (g_imag.astype(jnp.float32) + c_imag * (1.0 / 256)).astype(jnp.bfloat16)
            return carry

        lax.fori_loop(0, 4, one, 0)

    loads[0].wait()
    pack(0)
    pl.semaphore_wait(barrier, 255)
    send(packed, landed, 0, 0)
    loads[1].wait()
    pack(1)
    send(packed, landed, 1, 1)
    loads[2].wait()
    loads[3].wait()
    fill_factors()
    fill_tables()
    for h in range(HALVES):
        arrive(packed, landed, h, h)
        convolve(h)
        send(middle, back, h, 2 + h)
    for h in range(HALVES):
        arrive(middle, back, h, 2 + h)
        finish(h)
    for h in range(HALVES):
        leave(packed, landed, h, h)
        leave(middle, back, h, 2 + h)


def per_device(green, screened):
    blocks = pltpu.VMEM((HALVES, 256, 8, 256), jnp.bfloat16)
    matrices = jax.ShapeDtypeStruct((16, 256, 256), jnp.bfloat16)
    sigma, dressed = pl.pallas_call(
        kernel,
        out_shape=(matrices, matrices),
        in_specs=[pl.BlockSpec(memory_space=pl.ANY)] * 2,
        out_specs=[pl.BlockSpec(memory_space=pltpu.VMEM)] * 2,
        scratch_shapes=[
            pltpu.VMEM((16, 256, 256), jnp.bfloat16),
            pltpu.VMEM((2, 512, 128), jnp.float32),
            pltpu.VMEM((2, 1024, 128), jnp.float32),
            pltpu.VMEM((2, 2048, 128), jnp.float32),
            blocks,
            blocks,
            blocks,
            blocks,
            pltpu.VMEM((1024, 1024), jnp.bfloat16),
            pltpu.VMEM((1024, 1024), jnp.bfloat16),
            pltpu.VMEM((1024, 512), jnp.bfloat16),
            pltpu.VMEM((1024, 512), jnp.bfloat16),
            pltpu.SemaphoreType.DMA((4,)),
            pltpu.SemaphoreType.DMA((4,)),
            pltpu.SemaphoreType.DMA((4,)),
        ],
        compiler_params=pltpu.CompilerParams(
            collective_id=0, has_side_effects=True, vmem_limit_bytes=44 * 2**20
        ),
    )(green.reshape(16, 256, 256), screened.reshape(512, 256))
    return sigma.reshape(green.shape), dressed.reshape(green.shape)


def solution(mesh):
    spread = P(None, None, "krow", "kcol", None, None)
    return jax.shard_map(
        per_device,
        mesh=mesh,
        in_specs=(spread, P(None, None, ("krow", "kcol"))),
        out_specs=(spread, spread),
        check_vma=False,
    )
```

profile of v0, /device:TPU:1, one launch (start us, length us, event | category | flops | bytes accessed | tf_op | source)
XLA Modules:
  0.0 118.1 jit_solution(12744604221482281882)
XLA Ops:
  0.6 0.0 copy-start
  0.6 1.6 %copy-done = bf16[4,2,1,2,256,256]{5,4,3,2,1,0:T(8,128)(2,1)S(1)} copy-done((bf16[4,2,1,2,256,256]{5,4,3,2,1,0:T(8,128)(2,1)S(1)}, bf16[4,2,1,2,256,256]{5,4,3,2,1,0:T(8,128)(2,1)}, u32[]{:S(2)}) %copy-start) | copy-done | bytes 2097176
  2.2 0.0 copy-start.1
  2.2 1.0 copy-done.1
  3.3 112.2 %shard_map.41 = (bf16[16,256,256]{2,1,0:T(8,128)(2,1)S(1)}, bf16[16,256,256]{2,1,0:T(8,128)(2,1)S(1)}) custom-call(bf16[16,256,256]{2,1,0:T(8,128)(2,1)S(1)} %bitcast.8, f32[512,256]{1,0:T(8,128)S(1)} %bitcast.11), custom_call_target="tpu_custom_call" | custom-call | tf_op jit(solution)/shard_map/pallas_call | solution.py:236
  115.5 1.3 %copy.8 = bf16[4,2,1,2,256,256]{5,4,3,2,1,0:T(8,128)(2,1)} copy(bf16[4,2,1,2,256,256]{5,4,3,2,1,0:T(8,128)(2,1)S(1)} %bitcast.10) | data formatting | bytes 4194304
  116.8 1.3 %copy.9 = bf16[4,2,1,2,256,256]{5,4,3,2,1,0:T(8,128)(2,1)} copy(bf16[4,2,1,2,256,256]{5,4,3,2,1,0:T(8,128)(2,1)S(1)} %bitcast.9) | data formatting | bytes 4194304
Async XLA Ops:
  0.6 1.6 %copy-start = (bf16[4,2,1,2,256,256]{5,4,3,2,1,0:T(8,128)(2,1)S(1)}, bf16[4,2,1,2,256,256]{5,4,3,2,1,0:T(8,128)(2,1)}, u32[]{:S(2)}) copy-start(bf16[4,2,1,2,256,256]{5,4,3,2,1,0:T(8,128)(2,1)} %param.2) | copy-start | bytes 6291460
  2.2 1.0 copy-start.1
where the time goes:
time: 118 us
  Pallas kernels  112 us (95%)
  local copies, waits for them, and re-layouts  5.27 us (4%)
    pallas_call x1, Pallas kernels, per_device(): pl.pallas_call(kernel, out_shape=(matrices, matrices), in_specs=[pl.Block...  112 us
    unnamed x6, local copies, waits for them, and re-layouts  5.27 us

commit v1 on v0

--- a/solution.py
+++ b/solution.py
@@ -9,6 +9,7 @@
 
 MESH = pl.DeviceIdType.MESH
 HALVES = 2
+VMEM_LIMIT = 48 * 2**20
 SPLIT_TABLE = True
 SINE = [(-1) ** n * (math.pi / 16) ** (2 * n + 1) / math.factorial(2 * n + 1) for n in range(7)]
 
@@ -40,9 +41,55 @@
     lax.fori_loop(1, 32, body, 0)
 
 
+def for_peers_far_first(visit):
+    _, _, z, x, y, core = place()
+    z_rows = [((z + dz) % 8) * 4 for dz in range(8)]
+    x_rows = [(((x + dx) % 4) % 2) * 2 for dx in range(4)]
+    x_cols = [(((x + dx) % 4) // 2) * 4 for dx in range(4)]
+    y_cols = [(y + dy) % 4 for dy in range(4)]
+    cores = [core, 1 - core]
+    steps = [0, 1, 2, 1]
+    offsets = [(dz, dx, dy, dc) for dz in range(8) for dx in range(4) for dy in range(4) for dc in (1, 0)]
+    offsets.sort(key=lambda o: (-min(o[0], 8 - o[0]) - steps[o[1]] - steps[o[2]], o))
+    for dz, dx, dy, dc in offsets:
+        if (dz, dx, dy, dc) != (0, 0, 0, 0):
+            visit(z_rows[dz] + x_rows[dx] + cores[dc], x_cols[dx] + y_cols[dy])
+
+
+def dot(a, b):
+    return jnp.dot(a, b, preferred_element_type=jnp.float32)
+
+
+def unpack(back, wide, sigma):
+    def body(i, carry):
+        for side in range(2):
+            rows = back[pl.ds(i * 32, 32), :, pl.ds(side * 128, 128)].astype(jnp.float32)
+            wide[side, pl.ds(i * 256, 256), :] = rows.reshape(256, 128)
+        return carry
+
+    lax.fori_loop(0, 8, body, 0)
+    for j in range(8):
+        for side in range(2):
+            rows = wide[side, pl.ds(j, 256, stride=8), :]
+            sigma[j, :, pl.ds(side * 128, 128)] = rows.astype(jnp.bfloat16)
+
+
+def dress(green, sigma, dressed, real):
+    imag = real + 2
+    g_real, g_imag, s_real, s_imag = green[real], green[imag], sigma[real], sigma[imag]
+    g_lower, g_swapped = jnp.concatenate((g_real, g_imag), 0), jnp.concatenate((g_imag, g_real), 0)
+    k_real = dot(jnp.concatenate((g_real, -g_imag), 1), jnp.concatenate((s_real, s_imag), 0))
+    k_imag = dot(jnp.concatenate((g_real, g_imag), 1), jnp.concatenate((s_imag, s_real), 0))
+    k_real, k_imag = k_real.astype(jnp.bfloat16), k_imag.astype(jnp.bfloat16)
+    c_real = dot(jnp.concatenate((k_real, -k_imag), 1), g_lower)
+    c_imag = dot(jnp.concatenate((k_real, k_imag), 1), g_swapped)
+    dressed[real] = (g_real.astype(jnp.float32) + c_real * (1.0 / 256)).astype(jnp.bfloat16)
+    dressed[imag] = (g_imag.astype(jnp.float32) + c_imag * (1.0 / 256)).astype(jnp.bfloat16)
+
+
 def kernel(
-    green_hbm, screened_hbm, sigma, dressed,
-    green, weights, factors, wide, packed, landed, middle, back,
+    green_hbm, screened_hbm, sigma, dressed, green, last,
+    weights, factors, wide, packed, landed, middle, back,
     table, table_low, states, weighted, load_sem, send_sem, recv_sem,
 ):
     row, col = place()[:2]
@@ -61,7 +108,8 @@
     ]
     for load in loads:
         load.start()
-    for_peers(lambda r, c: pl.semaphore_signal(barrier, inc=1, device_id=(r, c), device_id_type=MESH))
+    with jax.named_scope("announce"):
+        for_peers_far_first(lambda r, c: pl.semaphore_signal(barrier, inc=1, device_id=(r, c), device_id_type=MESH))
 
     def pack(h):
         for j in range(8):
@@ -77,28 +125,22 @@
 
         lax.fori_loop(0, 8, body, 0)
 
-    def send(source, target, h, lane):
-        target[h, me] = source[h, me]
+    def send(source, target, lane):
+        target[me] = source[me]
 
         def one(r, c):
             pltpu.make_async_remote_copy(
-                source.at[h, r * 8 + c], target.at[h, me], send_sem.at[lane], recv_sem.at[lane],
+                source.at[r * 8 + c], target.at[me], send_sem.at[lane], recv_sem.at[lane],
                 device_id=(r, c), device_id_type=MESH,
             ).start()
 
         for_peers(one)
 
-    def arrive(source, target, h, lane):
-        pltpu.make_async_remote_copy(
-            source.at[h, pl.ds(0, 255)], target.at[h, pl.ds(0, 255)], send_sem.at[lane], recv_sem.at[lane],
+    def whole(source, target, lane):
+        return pltpu.make_async_remote_copy(
+            source.at[pl.ds(0, 255)], target.at[pl.ds(0, 255)], send_sem.at[lane], recv_sem.at[lane],
             device_id=(row, col), device_id_type=MESH,
-        ).wait_recv()
-
-    def leave(source, target, h, lane):
-        pltpu.make_async_remote_copy(
-            source.at[h, pl.ds(0, 255)], target.at[h, pl.ds(0, 255)], send_sem.at[lane], recv_sem.at[lane],
-            device_id=(row, col), device_id_type=MESH,
-        ).wait_send()
+        )
 
     def fill_tables():
         r = lax.broadcasted_iota(jnp.int32, (32, 1024), 0)
@@ -177,76 +219,101 @@
 
         lax.fori_loop(0, 4, inverse, 0)
 
-    def finish(h):
-        def unpack(i, carry):
-            for side in range(2):
-                rows = back[h, pl.ds(i * 32, 32), :, pl.ds(side * 128, 128)].astype(jnp.float32)
-                wide[side, pl.ds(i * 256, 256), :] = rows.reshape(256, 128)
-            return carry
-
-        lax.fori_loop(0, 8, unpack, 0)
-        for j in range(8):
-            for side in range(2):
-                rows = wide[side, pl.ds(j, 256, stride=8), :]
-                sigma[h * 8 + j, :, pl.ds(side * 128, 128)] = rows.astype(jnp.bfloat16)
-
-        def dot(a, b):
-            return jnp.dot(a, b, preferred_element_type=jnp.float32)
+    def finish():
+        unpack(back, wide, sigma)
 
         def one(i, carry):
-            real = h * 8 + (i // 2) * 4 + i % 2
-            imag = real + 2
-            g_real, g_imag, s_real, s_imag = green[real], green[imag], sigma[real], sigma[imag]
-            k_real = (dot(g_real, s_real) - dot(g_imag, s_imag)).astype(jnp.bfloat16)
-            k_imag = (dot(g_real, s_imag) + dot(g_imag, s_real)).astype(jnp.bfloat16)
-            c_real = dot(k_real, g_real) - dot(k_imag, g_imag)
-            c_imag = dot(k_real, g_imag) + dot(k_imag, g_real)
-            dressed[real] = (g_real.astype(jnp.float32) + c_real * (1.0 / 256)).astype(jnp.bfloat16)
-            dressed[imag] = (g_imag.astype(jnp.float32) + c_imag * (1.0 / 256)).astype(jnp.bfloat16)
+            dress(green, sigma, dressed, (i // 2) * 4 + i % 2)
             return carry
 
         lax.fori_loop(0, 4, one, 0)
 
-    loads[0].wait()
-    pack(0)
-    pl.semaphore_wait(barrier, 255)
-    send(packed, landed, 0, 0)
-    loads[1].wait()
-    pack(1)
-    send(packed, landed, 1, 1)
-    loads[2].wait()
-    loads[3].wait()
-    fill_factors()
-    fill_tables()
+    scope = jax.named_scope
+    with scope("load0"):
+        loads[0].wait()
+    with scope("pack0"):
+        pack(0)
+    with scope("barrier"):
+        pl.semaphore_wait(barrier, 255)
+    moves = [(packed.at[h], landed.at[h], h) for h in range(HALVES)]
+    moves += [(middle.at[h], (back, last)[h], 2 + h) for h in range(HALVES)]
+    with scope("send0"):
+        send(*moves[0])
+    with scope("load1"):
+        loads[1].wait()
+    with scope("pack1"):
+        pack(1)
+    with scope("send1"):
+        send(*moves[1])
+    with scope("factors"):
+        loads[2].wait()
+        loads[3].wait()
+        fill_factors()
+    with scope("tables"):
+        fill_tables()
     for h in range(HALVES):
-        arrive(packed, landed, h, h)
-        convolve(h)
-        send(middle, back, h, 2 + h)
-    for h in range(HALVES):
-        arrive(middle, back, h, 2 + h)
-        finish(h)
-    for h in range(HALVES):
-        leave(packed, landed, h, h)
-        leave(middle, back, h, 2 + h)
+        with scope(f"arrive{h}"):
+            whole(*moves[h]).wait_recv()
+        with scope(f"convolve{h}"):
+            convolve(h)
+        with scope(f"return{h}"):
+            send(*moves[2 + h])
+    with scope("back0"):
+        whole(*moves[2]).wait_recv()
+    with scope("finish0"):
+        finish()
+    with scope("back1"):
+        whole(*moves[3]).wait_recv()
+    with scope("leave"):
+        for move in moves:
+            whole(*move).wait_send()
+
+
+def closing(
+    sigma_half, dressed_half, green, last, sigma_hbm, dressed_hbm, wide, sigma, dressed, copy_sem
+):
+    def copy(source, target, part, lane):
+        return pltpu.make_async_copy(source, target.at[pl.ds(part, source.shape[0])], copy_sem.at[lane])
+
+    copies = [copy(sigma_half, sigma_hbm, 0, 0), copy(dressed_half, dressed_hbm, 0, 1)]
+    for c in copies:
+        c.start()
+    with jax.named_scope("unpack"):
+        unpack(last, wide, sigma)
+    copies.append(copy(sigma, sigma_hbm, 8, 2))
+    copies[-1].start()
+    for n in range(4):
+        real = (n // 2) * 4 + n % 2
+        with jax.named_scope(f"dress{n}"):
+            dress(green.at[pl.ds(8, 8)], sigma, dressed, real)
+        for part in (real, real + 2):
+            copies.append(copy(dressed.at[pl.ds(part, 1)], dressed_hbm, 8 + part, 3 + part))
+            copies[-1].start()
+    with jax.named_scope("drain"):
+        for c in copies:
+            c.wait()
 
 
 def per_device(green, screened):
+    vmem = pl.BlockSpec(memory_space=pltpu.VMEM)
+    hbm = pl.BlockSpec(memory_space=pltpu.HBM)
     blocks = pltpu.VMEM((HALVES, 256, 8, 256), jnp.bfloat16)
+    half = jax.ShapeDtypeStruct((8, 256, 256), jnp.bfloat16)
     matrices = jax.ShapeDtypeStruct((16, 256, 256), jnp.bfloat16)
-    sigma, dressed = pl.pallas_call(
+    wide = pltpu.VMEM((2, 2048, 128), jnp.float32)
+    parts = pl.pallas_call(
         kernel,
-        out_shape=(matrices, matrices),
-        in_specs=[pl.BlockSpec(memory_space=pl.ANY)] * 2,
-        out_specs=[pl.BlockSpec(memory_space=pltpu.VMEM)] * 2,
+        out_shape=(half, half, matrices, jax.ShapeDtypeStruct((256, 8, 256), jnp.bfloat16)),
+        in_specs=[hbm] * 2,
+        out_specs=[vmem] * 4,
         scratch_shapes=[
-            pltpu.VMEM((16, 256, 256), jnp.bfloat16),
             pltpu.VMEM((2, 512, 128), jnp.float32),
             pltpu.VMEM((2, 1024, 128), jnp.float32),
-            pltpu.VMEM((2, 2048, 128), jnp.float32),
+            wide,
             blocks,
             blocks,
             blocks,
-            blocks,
+            pltpu.VMEM((256, 8, 256), jnp.bfloat16),
             pltpu.VMEM((1024, 1024), jnp.bfloat16),
             pltpu.VMEM((1024, 1024), jnp.bfloat16),
             pltpu.VMEM((1024, 512), jnp.bfloat16),
@@ -256,9 +323,22 @@
             pltpu.SemaphoreType.DMA((4,)),
         ],
         compiler_params=pltpu.CompilerParams(
-            collective_id=0, has_side_effects=True, vmem_limit_bytes=44 * 2**20
+            collective_id=0, has_side_effects=True, vmem_limit_bytes=VMEM_LIMIT
         ),
-    )(green.reshape(16, 256, 256), screened.reshape(512, 256))
+    )(green.reshape(16, 256, 256), pltpu.with_memory_space_constraint(screened.reshape(512, 256), pltpu.HBM))
+    sigma, dressed = pl.pallas_call(
+        closing,
+        out_shape=(matrices, matrices),
+        in_specs=[vmem] * 4,
+        out_specs=[hbm] * 2,
+        scratch_shapes=[
+            wide,
+            pltpu.VMEM((8, 256, 256), jnp.bfloat16),
+            pltpu.VMEM((8, 256, 256), jnp.bfloat16),
+            pltpu.SemaphoreType.DMA((11,)),
+        ],
+        compiler_params=pltpu.CompilerParams(vmem_limit_bytes=16 * 2**20),
+    )(*parts)
     return sigma.reshape(green.shape), dressed.reshape(green.shape)
 
 

time: 118 us -> 111 us (0.941)
  local copies, waits for them, and re-layouts: 5.27 us -> 0 us
  Pallas kernels: 112 us -> 110 us
    unnamed x6 -> x0, local copies, waits for them, and re-layouts: 5.27 us -> none
    pallas_call x1 -> x2, Pallas kernels: 112 us -> 110 us  [the longest x1 107 us: per_device(): pl.pallas_call(kernel, out_shape=(half, half, matrices, jax.ShapeDtypeStr...]
where the time goes in v1:
time: 111 us
  Pallas kernels  110 us (99%)
    pallas_call x1, Pallas kernels, per_device(): pl.pallas_call(kernel, out_shape=(half, half, matrices, jax.ShapeDtypeStr...  107 us
    pallas_call x1, Pallas kernels, per_device(): pl.pallas_call(closing, out_shape=(matrices, matrices), in_specs=[vmem] *...  2.81 us

profile of v1, /device:TPU:1, one launch (start us, length us, event | category | flops | bytes accessed | tf_op | source)
XLA Modules:
  0.0 110.7 jit_solution(14946592857661753691)
XLA Ops:
  0.6 107.3 %shard_map.41 = (bf16[8,256,256]{2,1,0:T(8,128)(2,1)S(1)}, bf16[8,256,256]{2,1,0:T(8,128)(2,1)S(1)}, bf16[16,256,256]{2,1,0:T(8,128)(2,1)S(1)}, bf16[256,8,256]{2,1,0:T(8,128)(2,1)S(1)}) custom-call(bf16[16,256,256]{2,1,0:T(8,128)(2,1)} %bitcast.8, f32[512,256]{1,0:T(8,128)} %bitcast.9), custom_call_target="tpu_custom_call" | custom-call | tf_op jit(solution)/shard_map/pallas_call | solution.py:304
  107.9 2.8 %shard_map.42 = (bf16[16,256,256]{2,1,0:T(8,128)(2,1)}, bf16[16,256,256]{2,1,0:T(8,128)(2,1)}) custom-call(bf16[8,256,256]{2,1,0:T(8,128)(2,1)S(1)} %get-tuple-element.8.sigma_half, bf16[8,256,256]{2,1,0:T(8,128)(2,1)S(1)} %get-tuple-element.9.dressed_half, bf16[16,256,256]{2,1,0:T(8,128)(2,1)S(1)} %get-tuple-element.10.green, ...), custom_call_target="tpu_custom_call" | custom-call | tf_op jit(solution)/shard_map/pallas_call | solution.py:329

commit v2 on v1

--- a/solution.py
+++ b/solution.py
@@ -26,8 +26,7 @@
     z_rows = [((z + dz) % 8) * 4 for dz in (4, 1, 7, 2, 6, 3, 5, 0)]
 
     def group(step, first):
-        offset = (step * 13) % 32
-        x_to, y_to, core_to = (x + offset // 8) % 4, (y + (offset // 2) % 4) % 4, (core + offset % 2) % 2
+        x_to, y_to, core_to = (x + step // 8) % 4, (y + (step // 2) % 4) % 4, (core + step % 2) % 2
         low, col = (x_to % 2) * 2 + core_to, (x_to // 2) * 4 + y_to
         for z_row in z_rows[: 7 if first else 8]:
             visit(z_row + low, col)

time: 111 us -> 110 us (level)
    pallas_call x1, Pallas kernels: 107 us -> 106 us  [per_device(): pl.pallas_call(kernel, out_shape=(half, half, matrices, jax.ShapeDtypeStr...]
where the time goes in v2:
time: 110 us
  Pallas kernels  109 us (99%)
    pallas_call x1, Pallas kernels, per_device(): pl.pallas_call(kernel, out_shape=(half, half, matrices, jax.ShapeDtypeStr...  106 us
    pallas_call x1, Pallas kernels, per_device(): pl.pallas_call(closing, out_shape=(matrices, matrices), in_specs=[vmem] *...  2.81 us

profile of v2, /device:TPU:1, one launch (start us, length us, event | category | flops | bytes accessed | tf_op | source)
XLA Modules:
  0.0 109.6 jit_solution(11491993065914485330)
XLA Ops:
  0.6 106.1 %shard_map.41 = (bf16[8,256,256]{2,1,0:T(8,128)(2,1)S(1)}, bf16[8,256,256]{2,1,0:T(8,128)(2,1)S(1)}, bf16[16,256,256]{2,1,0:T(8,128)(2,1)S(1)}, bf16[256,8,256]{2,1,0:T(8,128)(2,1)S(1)}) custom-call(bf16[16,256,256]{2,1,0:T(8,128)(2,1)} %bitcast.8, f32[512,256]{1,0:T(8,128)} %bitcast.9), custom_call_target="tpu_custom_call" | custom-call | tf_op jit(solution)/shard_map/pallas_call | solution.py:303
  106.8 2.8 %shard_map.42 = (bf16[16,256,256]{2,1,0:T(8,128)(2,1)}, bf16[16,256,256]{2,1,0:T(8,128)(2,1)}) custom-call(bf16[8,256,256]{2,1,0:T(8,128)(2,1)S(1)} %get-tuple-element.8.sigma_half, bf16[8,256,256]{2,1,0:T(8,128)(2,1)S(1)} %get-tuple-element.9.dressed_half, bf16[16,256,256]{2,1,0:T(8,128)(2,1)S(1)} %get-tuple-element.10.green, ...), custom_call_target="tpu_custom_call" | custom-call | tf_op jit(solution)/shard_map/pallas_call | solution.py:328

commit v3 on v2

--- a/solution.py
+++ b/solution.py
@@ -277,16 +277,29 @@
     copies = [copy(sigma_half, sigma_hbm, 0, 0), copy(dressed_half, dressed_hbm, 0, 1)]
     for c in copies:
         c.start()
-    with jax.named_scope("unpack"):
-        unpack(last, wide, sigma)
-    copies.append(copy(sigma, sigma_hbm, 8, 2))
-    copies[-1].start()
-    for n in range(4):
-        real = (n // 2) * 4 + n % 2
-        with jax.named_scope(f"dress{n}"):
-            dress(green.at[pl.ds(8, 8)], sigma, dressed, real)
+    for i in range(8):
+        for side in range(2):
+            rows = last[pl.ds(i * 32, 32), :, pl.ds(side * 128, 128)].astype(jnp.float32)
+            wide[side, pl.ds(i * 256, 256), :] = rows.reshape(256, 128)
+
+    def take(j):
+        for side in range(2):
+            rows = wide[side, pl.ds(j, 256, stride=8), :]
+            sigma[j, :, pl.ds(side * 128, 128)] = rows.astype(jnp.bfloat16)
+
+    reals = (0, 1, 4, 5)
+    take(0)
+    take(2)
+    for n, real in enumerate(reals):
+        if n < 3:
+            take(reals[n + 1])
+            take(reals[n + 1] + 2)
+        dress(green.at[pl.ds(8, 8)], sigma, dressed, real)
         for part in (real, real + 2):
             copies.append(copy(dressed.at[pl.ds(part, 1)], dressed_hbm, 8 + part, 3 + part))
+            copies[-1].start()
+        if n == 2:
+            copies.append(copy(sigma, sigma_hbm, 8, 2))
             copies[-1].start()
     with jax.named_scope("drain"):
         for c in copies:

time: 110 us -> 110 us (level)
  no operation moved by 1% of the time
where the time goes in v3:
time: 110 us
  Pallas kernels  109 us (99%)
    pallas_call x1, Pallas kernels, per_device(): pl.pallas_call(kernel, out_shape=(half, half, matrices, jax.ShapeDtypeStr...  106 us
    pallas_call x1, Pallas kernels, per_device(): pl.pallas_call(closing, out_shape=(matrices, matrices), in_specs=[vmem] *...  2.72 us

profile of v3, /device:TPU:1, one launch (start us, length us, event | category | flops | bytes accessed | tf_op | source)
XLA Modules:
  0.0 109.5 jit_solution(6993408145699140268)
XLA Ops:
  0.6 106.1 %shard_map.41 = (bf16[8,256,256]{2,1,0:T(8,128)(2,1)S(1)}, bf16[8,256,256]{2,1,0:T(8,128)(2,1)S(1)}, bf16[16,256,256]{2,1,0:T(8,128)(2,1)S(1)}, bf16[256,8,256]{2,1,0:T(8,128)(2,1)S(1)}) custom-call(bf16[16,256,256]{2,1,0:T(8,128)(2,1)} %bitcast.8, f32[512,256]{1,0:T(8,128)} %bitcast.9), custom_call_target="tpu_custom_call" | custom-call | tf_op jit(solution)/shard_map/pallas_call | solution.py:316
  106.8 2.7 %shard_map.42 = (bf16[16,256,256]{2,1,0:T(8,128)(2,1)}, bf16[16,256,256]{2,1,0:T(8,128)(2,1)}) custom-call(bf16[8,256,256]{2,1,0:T(8,128)(2,1)S(1)} %get-tuple-element.8.sigma_half, bf16[8,256,256]{2,1,0:T(8,128)(2,1)S(1)} %get-tuple-element.9.dressed_half, bf16[16,256,256]{2,1,0:T(8,128)(2,1)S(1)} %get-tuple-element.10.green, ...), custom_call_target="tpu_custom_call" | custom-call | tf_op jit(solution)/shard_map/pallas_call | solution.py:341
